TPU v7x, 32 devices: a whole 2x2x4 slice. The times are simulated.
32 devices in a mesh: gx: 8 (over z, x), gy: 4 (over y, core).
Axes of the slice: x: 2, y: 2, z: 4, core: 2. Of those that a mesh axis runs over, the one named last changes fastest.
Arguments:
- velocity: float32 [3, 8192, 512], P(None, ('gx', 'gy')), may hold values from -6 to 6
- positions: float32 [3, 1024, 256], P(None, ('gx', 'gy')), may hold values from -6 to 6
- stiff_h: float32 [1024, 256], P(('gx', 'gy')), may hold values from 0.1 to 1
- stiff_v: float32 [1024, 256], P(('gx', 'gy')), may hold values from 0.1 to 1
- marker_owner: int32 [262144, 1], P(('gx', 'gy')), may hold values from 0 to 31; in each aligned block of 8192 rows (0 to 8191, 8192 to 16383, ...) at most 384 rows name the same one
- marker_element: int32 [262144], P(('gx', 'gy')), may hold values from 0 to 255
- marker_coords: float32 [3, 262144], P(None, ('gx', 'gy')), may hold values from -1 to 1
Outputs:
- new_positions: float32 [3, 1024, 256], P(None, ('gx', 'gy'))
- node_forces: float32 [3, 8192, 512], P(None, ('gx', 'gy'))
Inputs may be any that keep to these rules, and one draw needn't show every extreme that they name: `marker_owner`: among the markers of one device's rows, no owner is named more than 384 times, and in some devices' rows one owner is named exactly 384 times.
All inputs are finite; a program needn't handle non-finite values.
Results may differ from a plain program's by a relative error of at most 0.00013.
Values sent between devices are 32-bit elements; how exact they have to be, the bound alone decides.
No kernel may reach another device: no remote copies, remote signals or barrier semaphores. Data moves between devices by JAX's collectives and lax.ppermute only.
A program may use at most 64 MiB of HBM per device.

v0:
```python
import math
import jax
import jax.numpy as jnp
from jax import lax
from jax.sharding import PartitionSpec as P

POINTS = 8
bend_modulus = 0.05
time_step = 0.5


def padded(cells, sides, width):
    for axis, dim in sides:
        count = lax.axis_size(axis)
        head = lax.slice_in_dim(cells, 0, width, axis=dim)
        tail = lax.slice_in_dim(cells, cells.shape[dim] - width, cells.shape[dim], axis=dim)
        cells = jnp.concatenate(
            [
                lax.ppermute(tail, axis, [(i, (i + 1) % count) for i in range(count)]),
                cells,
                lax.ppermute(head, axis, [((i + 1) % count, i) for i in range(count)]),
            ],
            axis=dim,
        )
    return cells


def basis(values):
    abscissa = -jnp.cos(jnp.pi * jnp.arange(POINTS).astype(values.dtype) / (POINTS - 1))
    collected = []
    for i in range(POINTS):
        product = jnp.ones_like(values)
        for j in range(POINTS):
            if j != i:
                product = product * ((values - abscissa[j]) / (abscissa[i] - abscissa[j]))
        collected.append(product)
    return jnp.stack(collected)


def weight_table(factors):
    along_r = factors[0:POINTS].T
    along_s = factors[POINTS : 2 * POINTS].T
    along_t = factors[2 * POINTS : 3 * POINTS].T
    table = along_r[:, :, None, None] * along_s[:, None, :, None] * along_t[:, None, None, :]
    return table.reshape(along_r.shape[0], POINTS * POINTS * POINTS)


def surface_laplacian(extended):
    middle = extended[:, 1:-1]
    return (
        extended[:, 2:]
        + extended[:, :-2]
        + jnp.roll(middle, 1, axis=2)
        + jnp.roll(middle, -1, axis=2)
        - 4.0 * middle
    )


def tension(extended, stiff_h):
    points = extended[:3]
    vertical = extended[3]
    middle = points[:, 1:-1]
    return (
        stiff_h * (jnp.roll(middle, -1, axis=2) - middle)
        + jnp.roll(stiff_h, 1, axis=1) * (jnp.roll(middle, 1, axis=2) - middle)
        + vertical[1:-1] * (points[:, 2:] - middle)
        + vertical[:-2] * (points[:, :-2] - middle)
    )


def three_factors(coords):
    return jnp.concatenate([basis(coords[0]), basis(coords[1]), basis(coords[2])], axis=0)


def selector_of(block_elements, elem_count):
    return (block_elements[:, None] == jnp.arange(elem_count, dtype=jnp.int32)[None, :]).astype(
        jnp.float32
    )


def local(velocity, positions, stiff_h, stiff_v, marker_owner, marker_element, marker_coords):
    major_count = lax.axis_size("gx")
    minor_count = lax.axis_size("gy")
    devices_all = major_count * minor_count
    marker_count = marker_owner.shape[0]
    capacity = 3 * marker_count // (2 * devices_all)
    slot_total = devices_all * capacity
    elem_count = velocity.shape[1]
    stacked = jnp.concatenate([positions, stiff_v[None]], axis=0)
    extended = padded(stacked, ((("gx", "gy"), 1),), 1)
    pulling = tension(extended, stiff_h)
    laplace = surface_laplacian(extended[:3])
    laplace_wide = padded(laplace, ((("gx", "gy"), 1),), 1)
    bending = -bend_modulus * surface_laplacian(laplace_wide)
    marker_force = (pulling + bending).reshape(3, marker_count)
    owners = marker_owner[:, 0]
    ordering = jnp.argsort(owners, stable=True)
    sorted_owners = owners[ordering]
    offsets = jnp.searchsorted(sorted_owners, jnp.arange(devices_all, dtype=jnp.int32), side="left")
    within = jnp.arange(marker_count, dtype=jnp.int32) - offsets[sorted_owners]
    places = (
        jnp.zeros((marker_count,), jnp.int32).at[ordering].set(sorted_owners * capacity + within)
    )
    described = three_factors(marker_coords)
    lead = described.shape[0]
    payload = jnp.concatenate([described, marker_force], axis=0)
    width_all = payload.shape[0]
    outgoing = jnp.zeros((width_all, slot_total), jnp.float32).at[:, places].set(payload)
    slot_ids = jnp.zeros((1, slot_total), jnp.int32).at[:, places].set(marker_element[None])
    got_floats, got_slots = (
        lax.all_to_all(
            lax.all_to_all(
                outgoing.reshape(width_all, major_count, minor_count, capacity),
                "gx",
                split_axis=1,
                concat_axis=1,
                tiled=True,
            ),
            "gy",
            split_axis=2,
            concat_axis=2,
            tiled=True,
        ),
        lax.all_to_all(
            lax.all_to_all(
                slot_ids.reshape(1, major_count, minor_count, capacity),
                "gx",
                split_axis=1,
                concat_axis=1,
                tiled=True,
            ),
            "gy",
            split_axis=2,
            concat_axis=2,
            tiled=True,
        ),
    )
    got_floats = got_floats.reshape(width_all, slot_total)
    element_ids = got_slots.reshape(slot_total)
    factors = got_floats[:lead]
    pushes = got_floats[lead:]
    block_len = math.gcd(slot_total, 512)
    block_count = slot_total // block_len
    factor_blocks = factors.reshape(3 * POINTS, block_count, block_len).transpose(1, 0, 2)
    element_blocks = element_ids.reshape(block_count, block_len)
    push_blocks = pushes.reshape(3, block_count, block_len).transpose(1, 0, 2)

    def sample(inputs):
        block_factors, block_elements = inputs
        weights = weight_table(block_factors)
        selector = selector_of(block_elements, elem_count)
        gathered = jnp.einsum("be,ken->kbn", selector, velocity, precision=lax.Precision.HIGHEST)
        return jnp.sum(gathered * weights[None], axis=-1)

    sampled = lax.map(sample, (factor_blocks, element_blocks))
    returning = sampled.transpose(1, 0, 2).reshape(3, slot_total)
    arrived = lax.all_to_all(
        lax.all_to_all(
            returning.reshape(3, major_count, minor_count, capacity),
            "gx",
            split_axis=1,
            concat_axis=1,
            tiled=True,
        ),
        "gy",
        split_axis=2,
        concat_axis=2,
        tiled=True,
    )

    def deposit(running, inputs):
        block_factors, block_elements, block_pushes = inputs
        weights = weight_table(block_factors)
        selector = selector_of(block_elements, elem_count)
        loads = block_pushes[:, :, None] * weights[None]
        added = jnp.einsum("be,kbn->ken", selector, loads, precision=lax.Precision.HIGHEST)
        return (running + added, None)

    node_forces, unused = lax.scan(
        deposit, jnp.zeros_like(velocity), (factor_blocks, element_blocks, push_blocks)
    )
    moved = jnp.take(arrived.reshape(3, slot_total), places, axis=1).reshape(positions.shape)
    return (positions + time_step * moved, node_forces)


def solution(mesh):
    return jax.shard_map(
        local,
        mesh=mesh,
        in_specs=(
            P(None, ("gx", "gy"), None),
            P(None, ("gx", "gy"), None),
            P(("gx", "gy"), None),
            P(("gx", "gy"), None),
            P(("gx", "gy"), None),
            P(("gx", "gy")),
            P(None, ("gx", "gy")),
        ),
        out_specs=(P(None, ("gx", "gy"), None), P(None, ("gx", "gy"), None)),
        check_vma=False,
    )
```

profile of v0, /device:TPU:0, one launch (start us, length us, event | category | flops | bytes accessed | tf_op | source)
XLA Modules:
  0.0 586.4 jit_solution(10198000036078593590)
XLA Ops:
  2.0 6.0 %collective-permute-start = (f32[4,1,256]{2,1,0:T(1,128)S(1)}, f32[4,1,256]{2,1,0:T(1,128)S(1)}, u32[]{:S(2)}, u32[]{:S(2)}) collective-permute-start(f32[4,1,256]{2,1,0:T(1,128)S(1)} %get-tuple-element.267), channel_id=1, source_target_pairs={{1,0},{2,1},{3,2},{4,3},{5,4},{6,5},{7,6},{8,7},{9,8},{10,9},{11,1... | collective-permute-start | bytes 12296 | tf_op jit(solution)/shard_map/ppermute | solution.py:21
  8.0 7.5 %sort.17 = (s32[8192]{0:T(1024)}, s32[8192]{0:T(1024)S(1)}) sort(s32[8192]{0:T(1024)} %bitcast.127, s32[8192]{0:T(1024)S(1)} %iota.23), dimensions={0}, to_apply=%region_0.1 | sort | flops 106496 | bytes 131072 | tf_op jit(solution)/shard_map/jit(argsort)/sort | solution.py:97
  15.5 45.5 %gather_fusion.1 = s32[8192]{0:T(1024)S(1)} fusion(s32[8192]{0:T(1024)S(1)} %bitcast.128, s32[8192]{0:T(1024)S(1)} %get-tuple-element.305), kind=kCustom, calls=%fused_computation.1 | custom fusion | bytes 98304 | tf_op jit(solution)/shard_map/gather | solution.py:98
  61.1 10.5 %while.46 = (s32[]{:T(128)}, u32[32]{0:T(128)S(1)}, u32[32]{0:T(128)S(1)}, s32[8192]{0:T(1024)S(1)}, s32[]{:T(128)}, /*index=5*/s32[]{:T(128)}, s32[]{}) while((s32[]{:T(128)}, u32[32]{0:T(128)S(1)}, u32[32]{0:T(128)S(1)}, s32[8192]{0:T(1024)S(1)}, s32[]{:T(128)}, /*index=5*/s32[]{:T(128)}, s32[]{}) %tuple.172), condition=%wide.region_2.3_spmd.clone, body=%wide.region_1.2_spmd.clone.sunk | while | flops 1444 | bytes 5732 | solution.py:99
  80.0 15.9 %fusion.35 = s32[8192]{0:T(1024)S(1)} fusion(pred[8192]{0:T(1024)(128)(4,1)S(1)} %get-tuple-element.228, pred[8192]{0:T(1024)(128)(4,1)S(1)} %get-tuple-element.227, pred[8192]{0:T(1024)(128)(4,1)S(1)} %get-tuple-element.226, pred[8192]{0:T(1024)(128)(4,1)S(1)} %get-tuple-element.225, pred[8192]{0:T(1024)(128)(4,1)S(1)} %get-tuple-element.224, ...), kind=kLoop, calls=%fused_computation.250 | loop fusion | flops 229376 | bytes 303204 | tf_op jit(solution)/shard_map/add | solution.py:102
  95.9 30.5 %scatter_custom_fusion = s32[8192]{0:T(1024)S(1)} fusion(s32[8192]{0:T(1024)S(1)} %get-tuple-element.306, s32[8192]{0:T(1024)S(1)} %fusion.35, s32[]{:T(128)} %constant.79.clone.1), kind=kCustom, calls=%fused_computation.280 | custom fusion | bytes 32772 | tf_op jit(solution)/shard_map/scatter | solution.py:102
  126.4 30.7 %scatter_custom_fusion.1 = s32[12288]{0:T(1024)S(1)} fusion(s32[8192]{0:T(1024)S(1)} %get-tuple-element.304, s32[8192]{0:T(1024)} %param.18, s32[]{:T(128)} %constant.79.clone.1), kind=kCustom, calls=%fused_computation.252 | custom fusion | bytes 49664 | tf_op jit(solution)/shard_map/scatter | solution.py:109
  231.5 4.8 divide_multiply_fusion
  236.3 4.9 divide_multiply_fusion.6
  241.2 4.9 divide_multiply_fusion.12
  246.1 4.9 divide_multiply_fusion.18
  250.9 4.9 divide_multiply_fusion.24
  255.8 4.9 divide_multiply_fusion.30
  260.7 4.8 divide_multiply_fusion.36
  265.5 4.9 divide_multiply_fusion.42
  274.9 5.3 collective-permute-done.3
  284.4 23.9 %scatter_custom_fusion.2 = f32[27,12288]{0,1:T(8,128)} fusion(s32[8192]{0:T(1024)S(1)} %get-tuple-element.304, f32[8192,27]{1,0:T(8,128)} %copy.89, f32[]{:T(128)} %constant.87.clone.1), kind=kCustom, calls=%fused_computation.41 | custom fusion | bytes 1327616 | tf_op jit(solution)/shard_map/scatter | solution.py:108
  308.2 5.5 copy.90
  318.0 26.6 %all-to-all-done.2 = f32[27,8,4,384]{3,2,0,1:T(4,128)S(1)} async-done(((f32[27,8,4,384]{3,2,0,1:T(4,128)}), f32[27,8,4,384]{3,2,0,1:T(4,128)S(1)}, u32[]{:S(2)}, u32[]{:S(2)}) %all-to-all-start.2) | async-done | bytes 1327136 | tf_op jit(solution)/shard_map/all_to_all | solution.py:112
  357.5 16.7 %all-to-all-done.3 = f32[27,8,4,384]{3,1,0,2:T(8,128)} async-done(((f32[27,8,4,384]{3,1,0,2:T(8,128)}), f32[27,8,4,384]{3,1,0,2:T(8,128)}, u32[]{:S(2)}, u32[]{:S(2)}) %all-to-all-start.3) | async-done | bytes 1327136 | tf_op jit(solution)/shard_map/all_to_all | solution.py:111
  380.9 64.9 %while.45 = (s32[]{:T(128)}, f32[24,3,512]{2,1,0:T(4,128)S(1)}, s32[24,512]{1,0:T(8,128)S(1)}, f32[3,256,512]{1,2,0:T(8,128)S(1)}, f32[24,24,512]{2,1,0:T(8,128)}, /*index=5*/s32[]{:T(128)}, s32[]{:T(128)}, s32[]{}, s32[]{}) while((s32[]{:T(128)}, f32[24,3,512]{2,1,0:T(4,128)S(1)}, s32[24,512]{1,0:T(8,128)S(1)}, f32[3,256,512]{1,2,0:T(8,128)S(1)}, ...), condition=%wide.region_8.9_spmd, body=%wide.region_6.8_spmd.sunk | while | flops 2417916416 | bytes 4108425 | solution.py:155
  451.5 6.4 %all-to-all-done.4 = f32[3,8,4,384]{3,2,0,1:T(4,128)S(1)} async-done(((f32[3,8,4,384]{3,2,0,1:T(4,128)}), f32[3,8,4,384]{3,2,0,1:T(4,128)S(1)}, u32[]{:S(2)}, u32[]{:S(2)}) %all-to-all-start.4) | async-done | bytes 147488 | tf_op jit(solution)/shard_map/all_to_all | solution.py:158
  461.8 85.0 %while.47 = (s32[]{:T(128)}, f32[3,256,512]{1,2,0:T(8,128)S(1)}, f32[24,3,512]{2,0,1:T(8,128)S(1)}, f32[24,24,512]{2,1,0:T(8,128)}, s32[24,512]{1,0:T(8,128)S(1)}, /*index=5*/s32[]{:T(128)}, s32[]{:T(128)}, s32[]{}, s32[]{}) while((s32[]{:T(128)}, f32[3,256,512]{1,2,0:T(8,128)S(1)}, f32[24,3,512]{2,0,1:T(8,128)S(1)}, ...), condition=%wide.region_10.11_spmd.clone, body=%wide.region_9.10_spmd.clone.sunk | while | flops 2417917952 | bytes 5689491 | solution.py:179
  552.4 30.5 %gather_fusion.2 = f32[8192,3]{1,0:T(8,128)} fusion(f32[3,12288]{0,1:T(8,128)} %bitcast.133, s32[8192]{0:T(1024)S(1)} %get-tuple-element.303), kind=kCustom, calls=%fused_computation.2 | custom fusion | bytes 229376 | tf_op jit(solution)/shard_map/jit(_take)/gather | solution.py:182
  (446 shorter events, 223.5 us)
Async XLA Ops:
  0.6 14.9 %copy-start = (s32[8192,1]{0,1:T(1,128)S(1)}, s32[8192,1]{0,1:T(1,128)}, u32[]{:S(2)}) copy-start(s32[8192,1]{0,1:T(1,128)} %param.17) | copy-start | bytes 98308
  1.4 269.1 %collective-permute-start.1 = (f32[4,1,256]{2,1,0:T(1,128)S(1)}, f32[4,1,256]{2,1,0:T(1,128)S(1)}, u32[]{:S(2)}, u32[]{:S(2)}) collective-permute-start(f32[4,1,256]{2,1,0:T(1,128)S(1)} %get-tuple-element.268), channel_id=1, source_target_pairs={{0,1},{1,2},{2,3},{3,4},{4,5},{5,6},{6,7},{7,8},{8,9},{9,10},{10,1... | collective-permute-start | bytes 12296 | tf_op jit(solution)/shard_map/ppermute | solution.py:19
  2.0 268.6 %collective-permute-start = (f32[4,1,256]{2,1,0:T(1,128)S(1)}, f32[4,1,256]{2,1,0:T(1,128)S(1)}, u32[]{:S(2)}, u32[]{:S(2)}) collective-permute-start(f32[4,1,256]{2,1,0:T(1,128)S(1)} %get-tuple-element.267), channel_id=1, source_target_pairs={{1,0},{2,1},{3,2},{4,3},{5,4},{6,5},{7,6},{8,7},{9,8},{10,9},{11,1... | collective-permute-start | bytes 12296 | tf_op jit(solution)/shard_map/ppermute | solution.py:21
  61.0 170.1 %copy-start.1 = (f32[3,32,256]{2,1,0:T(8,128)S(1)}, f32[3,32,256]{2,1,0:T(8,128)}, u32[]{:S(2)}) copy-start(f32[3,32,256]{2,1,0:T(8,128)} %param.14) | copy-start | bytes 294916
  71.6 159.8 %copy-start.5 = (f32[32,256]{1,0:T(8,128)S(1)}, f32[32,256]{1,0:T(8,128)}, u32[]{:S(2)}) copy-start(f32[32,256]{1,0:T(8,128)} %param.15) | copy-start | bytes 98308
  71.6 159.8 %copy-start.2 = (f32[3,8192]{1,0:T(4,128)S(1)}, f32[3,8192]{1,0:T(4,128)}, u32[]{:S(2)}) copy-start(f32[3,8192]{1,0:T(4,128)} %param.19) | copy-start | bytes 294916
  80.0 190.5 %copy-start.4 = (f32[32,256]{1,0:T(8,128)S(1)}, f32[32,256]{1,0:T(8,128)}, u32[]{:S(2)}) copy-start(f32[32,256]{1,0:T(8,128)} %param.16) | copy-start | bytes 98308
  157.8 156.0 %all-to-all-start = ((s32[1,8,4,384]{3,2,0,1:T(4,128)}), s32[1,8,4,384]{3,2,0,1:T(4,128)S(1)}, u32[]{:S(2)}, u32[]{:S(2)}) async-start(s32[1,8,4,384]{3,2,0,1:T(4,128)} %reshape.123), calls=%async_computation | async-start | bytes 98304 | tf_op jit(solution)/shard_map/all_to_all | solution.py:125
  270.9 4.0 collective-permute-start.2
  273.5 6.6 %collective-permute-start.3 = (f32[3,1,256]{2,1,0:T(1,128)S(1)}, f32[3,1,256]{2,1,0:T(1,128)S(1)}, u32[]{:S(2)}, u32[]{:S(2)}) collective-permute-start(f32[3,1,256]{2,1,0:T(1,128)S(1)} %get-tuple-element.298), channel_id=1, source_target_pairs={{0,1},{1,2},{2,3},{3,4},{4,5},{5,6},{6,7},{7,8},{8,9},{9,10},{10,1... | collective-permute-start | bytes 9224 | tf_op jit(solution)/shard_map/ppermute | solution.py:19
  313.8 30.8 %all-to-all-start.2 = ((f32[27,8,4,384]{3,2,0,1:T(4,128)}), f32[27,8,4,384]{3,2,0,1:T(4,128)S(1)}, u32[]{:S(2)}, u32[]{:S(2)}) async-start(f32[27,8,4,384]{3,2,0,1:T(4,128)} %copy.90), calls=%async_computation.2 | async-start | bytes 2654208 | tf_op jit(solution)/shard_map/all_to_all | solution.py:112
  344.6 7.8 %all-to-all-start.1 = ((s32[1,8,4,384]{3,1,0,2:T(8,128)}), s32[1,8,4,384]{3,1,0,2:T(8,128)S(1)}, u32[]{:S(2)}, u32[]{:S(2)}) async-start(s32[1,8,4,384]{3,1,0,2:T(8,128)} %copy.87), calls=%async_computation.1 | async-start | bytes 98304 | tf_op jit(solution)/shard_map/all_to_all | solution.py:124
  349.5 7.4 %copy-start.3 = (f32[3,256,512]{2,1,0:T(8,128)S(1)}, f32[3,256,512]{2,1,0:T(8,128)}, u32[]{:S(2)}) copy-start(f32[3,256,512]{2,1,0:T(8,128)} %param.13) | copy-start | bytes 4718596
  352.4 21.8 %all-to-all-start.3 = ((f32[27,8,4,384]{3,1,0,2:T(8,128)}), f32[27,8,4,384]{3,1,0,2:T(8,128)}, u32[]{:S(2)}, u32[]{:S(2)}) async-start(f32[27,8,4,384]{3,1,0,2:T(8,128)} %copy.91), calls=%async_computation.3 | async-start | bytes 2654208 | tf_op jit(solution)/shard_map/all_to_all | solution.py:111
  446.6 11.2 %all-to-all-start.4 = ((f32[3,8,4,384]{3,2,0,1:T(4,128)}), f32[3,8,4,384]{3,2,0,1:T(4,128)S(1)}, u32[]{:S(2)}, u32[]{:S(2)}) async-start(f32[3,8,4,384]{3,2,0,1:T(4,128)} %copy.96), calls=%async_computation.4 | async-start | bytes 294912 | tf_op jit(solution)/shard_map/all_to_all | solution.py:158
  458.5 90.0 %all-to-all-start.5 = ((f32[3,8,4,384]{3,1,0,2:T(8,128)}), f32[3,8,4,384]{3,1,0,2:T(8,128)S(1)}, u32[]{:S(2)}, u32[]{:S(2)}) async-start(f32[3,8,4,384]{3,1,0,2:T(8,128)} %copy.97), calls=%async_computation.5 | async-start | bytes 294912 | tf_op jit(solution)/shard_map/all_to_all | solution.py:157
where the time goes:
time: 596 us; the launch traced here: 586 us
  local copies, waits for them, and re-layouts  242 us (41%)
  matrix products  103 us (17%)
  other arithmetic  78.1 us (13%)
  between operations  70.2 us (12%)
  waiting for transfers between devices  59.2 us (10%)
  starting transfers between devices  31.7 us (5%)
    dot_general x24, matrix products, deposit(): jnp.einsum('be,kbn->ken', selector, loads, precision=lax.Precision.HIGHEST)  60.9 us
    gather x1, local copies, waits for them, and re-layouts, local(): sorted_owners = owners[ordering]  45.5 us
    dot_general x24, matrix products, sample(): jnp.einsum('be,ken->kbn', selector, velocity, precision=lax.Precision.HIG...  41.8 us
    mul x8, other arithmetic, basis(): product = product * ((values - abscissa[j]) / (abscissa[i] - abscissa[j]))  39 us
    transpose x48, local copies, waits for them, and re-layouts, weight_table(): along_r = factors[0:POINTS].T  36.7 us
    gather x2, local copies, waits for them, and re-layouts, local(): jnp.take(arrived.reshape(3, slot_total), places, axis=1)  33.3 us
    scatter x1, local copies, waits for them, and re-layouts, local(): jnp.zeros((1, slot_total), jnp.int32).at[:, places]  30.7 us
    scatter x1, local copies, waits for them, and re-layouts, local(): jnp.zeros((marker_count,), jnp.int32).at[ordering]  30.5 us
  transfers between devices with their start and end apart: 10, of which 6 were waited for; matrix products, arithmetic and copies ran while one was open for 53% of the time, Pallas kernels for 0%

commit v1 on v0

--- a/solution.py
+++ b/solution.py
@@ -7,6 +7,29 @@
 POINTS = 8
 bend_modulus = 0.05
 time_step = 0.5
+
+
+def split_up(value, dim, size):
+    lengths = value.shape
+    parts = value.reshape(*lengths[:dim], size, lengths[dim] // size, *lengths[dim + 1 :])
+    return jnp.moveaxis(parts, dim, 0)
+
+
+def joined_along(pieces, dim):
+    lengths = list(pieces.shape[1:])
+    lengths[dim] *= pieces.shape[0]
+    return jnp.moveaxis(pieces, 0, dim).reshape(lengths)
+
+
+def swapped_with_each(x, axis, split_dim, concat_dim):
+    size, index = (lax.axis_size(axis), lax.axis_index(axis))
+    blocks = split_up(x, split_dim, size)
+    finished = [blocks[index]]
+    for hop in range(1, size):
+        sent = blocks[index ^ hop]
+        finished.append(lax.ppermute(sent, axis, [(i, i ^ hop) for i in range(size)]))
+    blocks = jnp.stack(finished)[index ^ jnp.arange(size)]
+    return joined_along(blocks, concat_dim)
 
 
 def padded(cells, sides, width):
@@ -109,12 +132,8 @@
     slot_ids = jnp.zeros((1, slot_total), jnp.int32).at[:, places].set(marker_element[None])
     got_floats, got_slots = (
         lax.all_to_all(
-            lax.all_to_all(
-                outgoing.reshape(width_all, major_count, minor_count, capacity),
-                "gx",
-                split_axis=1,
-                concat_axis=1,
-                tiled=True,
+            swapped_with_each(
+                outgoing.reshape(width_all, major_count, minor_count, capacity), "gx", 1, 1
             ),
             "gy",
             split_axis=2,

time: 596 us -> 599 us (level)
  waiting for transfers between devices: 59.2 us -> 34.3 us
  local copies, waits for them, and re-layouts: 242 us -> 258 us
  starting transfers between devices: 31.7 us -> 43.4 us
    all_to_all x2 -> x1, waiting for transfers between devices: 43.3 us -> 16.9 us  [local(): lax.all_to_all(swapped_with_each(outgoing.reshape(width_all, major_count,...]
    another operation x0 -> x10, local copies, waits for them, and re-layouts: none -> 15.5 us
    ppermute x0 -> x7, starting transfers between devices: none -> 11.2 us  [swapped_with_each(): lax.ppermute(sent, axis, [(i, i ^ hop) for i in range(size)])]
  transfers between devices with their start and end apart: 10 -> 16, of which waited for: 6 -> 5; matrix products, arithmetic and copies ran while one was open for 53% -> 56% of each run, Pallas kernels for 0% -> 0%
where the time goes in v1:
time: 599 us; the launch traced here: 589 us
  local copies, waits for them, and re-layouts  258 us (43%)
  matrix products  103 us (17%)
  other arithmetic  78.1 us (13%)
  between operations  70.4 us (12%)
  starting transfers between devices  43.4 us (7%)
  waiting for transfers between devices  34.3 us (6%)
    dot_general x24, matrix products, deposit(): jnp.einsum('be,kbn->ken', selector, loads, precision=lax.Precision.HIGHEST)  60.9 us
    gather x1, local copies, waits for them, and re-layouts, local(): sorted_owners = owners[ordering]  45.5 us
    dot_general x24, matrix products, sample(): jnp.einsum('be,ken->kbn', selector, velocity, precision=lax.Precision.HIG...  41.8 us
    mul x8, other arithmetic, basis(): product = product * ((values - abscissa[j]) / (abscissa[i] - abscissa[j]))  39 us
    transpose x48, local copies, waits for them, and re-layouts, weight_table(): along_r = factors[0:POINTS].T  36.7 us
    gather x2, local copies, waits for them, and re-layouts, local(): jnp.take(arrived.reshape(3, slot_total), places, axis=1)  33.3 us
    scatter x1, local copies, waits for them, and re-layouts, local(): jnp.zeros((1, slot_total), jnp.int32).at[:, places]  30.7 us
    scatter x1, local copies, waits for them, and re-layouts, local(): jnp.zeros((marker_count,), jnp.int32).at[ordering]  30.5 us
  transfers between devices with their start and end apart: 16, of which 5 were waited for; matrix products, arithmetic and copies ran while one was open for 56% of the time, Pallas kernels for 0%

profile of v1, /device:TPU:0, one launch (start us, length us, event | category | flops | bytes accessed | tf_op | source)
XLA Modules:
  0.0 589.4 jit_solution(9434356705646395022)
XLA Ops:
  2.0 6.0 %collective-permute-start = (f32[4,1,256]{2,1,0:T(1,128)S(1)}, f32[4,1,256]{2,1,0:T(1,128)S(1)}, u32[]{:S(2)}, u32[]{:S(2)}) collective-permute-start(f32[4,1,256]{2,1,0:T(1,128)S(1)} %get-tuple-element.299), channel_id=1, source_target_pairs={{1,0},{2,1},{3,2},{4,3},{5,4},{6,5},{7,6},{8,7},{9,8},{10,9},{11,1... | collective-permute-start | bytes 12296 | tf_op jit(solution)/shard_map/ppermute | solution.py:44
  8.0 7.5 %sort.17 = (s32[8192]{0:T(1024)}, s32[8192]{0:T(1024)S(1)}) sort(s32[8192]{0:T(1024)} %bitcast.158, s32[8192]{0:T(1024)S(1)} %iota.27), dimensions={0}, to_apply=%region_0.1 | sort | flops 106496 | bytes 131072 | tf_op jit(solution)/shard_map/jit(argsort)/sort | solution.py:120
  15.5 45.5 %gather_fusion.1 = s32[8192]{0:T(1024)S(1)} fusion(s32[8192]{0:T(1024)S(1)} %bitcast.159, s32[8192]{0:T(1024)S(1)} %get-tuple-element.337), kind=kCustom, calls=%fused_computation.1 | custom fusion | bytes 98304 | tf_op jit(solution)/shard_map/gather | solution.py:121
  61.1 10.5 %while.46 = (s32[]{:T(128)}, u32[32]{0:T(128)S(1)}, u32[32]{0:T(128)S(1)}, s32[8192]{0:T(1024)S(1)}, s32[]{:T(128)}, /*index=5*/s32[]{:T(128)}, s32[]{}) while((s32[]{:T(128)}, u32[32]{0:T(128)S(1)}, u32[32]{0:T(128)S(1)}, s32[8192]{0:T(1024)S(1)}, s32[]{:T(128)}, /*index=5*/s32[]{:T(128)}, s32[]{}) %tuple.185), condition=%wide.region_2.3_spmd.clone, body=%wide.region_1.2_spmd.clone.sunk | while | flops 1444 | bytes 5732 | solution.py:122
  80.0 15.9 %fusion.35 = s32[8192]{0:T(1024)S(1)} fusion(pred[8192]{0:T(1024)(128)(4,1)S(1)} %get-tuple-element.252, pred[8192]{0:T(1024)(128)(4,1)S(1)} %get-tuple-element.251, pred[8192]{0:T(1024)(128)(4,1)S(1)} %get-tuple-element.250, pred[8192]{0:T(1024)(128)(4,1)S(1)} %get-tuple-element.249, pred[8192]{0:T(1024)(128)(4,1)S(1)} %get-tuple-element.248, ...), kind=kLoop, calls=%fused_computation.259 | loop fusion | flops 229376 | bytes 303204 | tf_op jit(solution)/shard_map/add | solution.py:125
  95.9 30.5 %scatter_custom_fusion = s32[8192]{0:T(1024)S(1)} fusion(s32[8192]{0:T(1024)S(1)} %get-tuple-element.338, s32[8192]{0:T(1024)S(1)} %fusion.35, s32[]{:T(128)} %constant.60.clone.1), kind=kCustom, calls=%fused_computation.289 | custom fusion | bytes 32772 | tf_op jit(solution)/shard_map/scatter | solution.py:125
  126.4 30.7 %scatter_custom_fusion.1 = s32[12288]{0:T(1024)S(1)} fusion(s32[8192]{0:T(1024)S(1)} %get-tuple-element.336, s32[8192]{0:T(1024)} %param.18, s32[]{:T(128)} %constant.60.clone.1), kind=kCustom, calls=%fused_computation.261 | custom fusion | bytes 49664 | tf_op jit(solution)/shard_map/scatter | solution.py:132
  231.5 4.8 divide_multiply_fusion
  236.4 4.9 divide_multiply_fusion.6
  241.3 4.9 divide_multiply_fusion.12
  246.1 4.9 divide_multiply_fusion.18
  251.0 4.9 divide_multiply_fusion.24
  255.9 4.9 divide_multiply_fusion.30
  260.8 4.8 divide_multiply_fusion.36
  265.6 4.9 divide_multiply_fusion.42
  274.9 5.3 collective-permute-done.3
  284.4 23.9 %scatter_custom_fusion.2 = f32[27,12288]{0,1:T(8,128)} fusion(s32[8192]{0:T(1024)S(1)} %get-tuple-element.336, f32[8192,27]{1,0:T(8,128)} %copy.162, f32[]{:T(128)} %constant.101.clone.1), kind=kCustom, calls=%fused_computation.42 | custom fusion | bytes 1327616 | tf_op jit(solution)/shard_map/scatter | solution.py:131
  335.3 5.3 collective-permute-start.10
  355.6 16.9 %all-to-all-done.2 = f32[27,8,4,384]{3,1,0,2:T(8,128)} async-done(((f32[27,8,4,384]{3,1,0,2:T(8,128)}), f32[27,8,4,384]{3,1,0,2:T(8,128)}, u32[]{:S(2)}, u32[]{:S(2)}) %all-to-all-start.2) | async-done | bytes 1327136 | tf_op jit(solution)/shard_map/all_to_all | solution.py:134
  379.3 64.9 %while.45 = (s32[]{:T(128)}, f32[24,3,512]{2,1,0:T(4,128)S(1)}, s32[24,512]{1,0:T(8,128)S(1)}, f32[3,256,512]{1,2,0:T(8,128)S(1)}, f32[24,24,512]{2,1,0:T(8,128)}, /*index=5*/s32[]{:T(128)}, s32[]{:T(128)}, s32[]{}, s32[]{}) while((s32[]{:T(128)}, f32[24,3,512]{2,1,0:T(4,128)S(1)}, s32[24,512]{1,0:T(8,128)S(1)}, f32[3,256,512]{1,2,0:T(8,128)S(1)}, ...), condition=%wide.region_8.9_spmd, body=%wide.region_6.8_spmd.sunk | while | flops 2417916416 | bytes 4108425 | solution.py:174
  445.0 8.2 %all-to-all-start.3 = ((f32[3,8,4,384]{3,2,0,1:T(4,128)}), f32[3,8,4,384]{3,2,0,1:T(4,128)S(1)}, u32[]{:S(2)}, u32[]{:S(2)}) async-start(f32[3,8,4,384]{3,2,0,1:T(4,128)} %copy.176), calls=%async_computation.3 | async-start | bytes 294912 | tf_op jit(solution)/shard_map/all_to_all | solution.py:177
  454.3 6.4 %all-to-all-done.3 = f32[3,8,4,384]{3,2,0,1:T(4,128)S(1)} async-done(((f32[3,8,4,384]{3,2,0,1:T(4,128)}), f32[3,8,4,384]{3,2,0,1:T(4,128)S(1)}, u32[]{:S(2)}, u32[]{:S(2)}) %all-to-all-start.3) | async-done | bytes 147488 | tf_op jit(solution)/shard_map/all_to_all | solution.py:177
  464.9 85.0 %while.47 = (s32[]{:T(128)}, f32[3,256,512]{1,2,0:T(8,128)S(1)}, f32[24,3,512]{2,0,1:T(8,128)S(1)}, f32[24,24,512]{2,1,0:T(8,128)}, s32[24,512]{1,0:T(8,128)S(1)}, /*index=5*/s32[]{:T(128)}, s32[]{:T(128)}, s32[]{}, s32[]{}) while((s32[]{:T(128)}, f32[3,256,512]{1,2,0:T(8,128)S(1)}, f32[24,3,512]{2,0,1:T(8,128)S(1)}, ...), condition=%wide.region_10.11_spmd.clone, body=%wide.region_9.10_spmd.clone.sunk | while | flops 2417917952 | bytes 5689491 | solution.py:198
  555.4 30.5 %gather_fusion.3 = f32[8192,3]{1,0:T(8,128)} fusion(f32[3,12288]{0,1:T(8,128)} %bitcast.164, s32[8192]{0:T(1024)S(1)} %get-tuple-element.335), kind=kCustom, calls=%fused_computation.3 | custom fusion | bytes 229376 | tf_op jit(solution)/shard_map/jit(_take)/gather | solution.py:201
  (481 shorter events, 244.7 us)
Async XLA Ops:
  0.6 14.9 %copy-start = (s32[8192,1]{0,1:T(1,128)S(1)}, s32[8192,1]{0,1:T(1,128)}, u32[]{:S(2)}) copy-start(s32[8192,1]{0,1:T(1,128)} %param.17) | copy-start | bytes 98308
  1.4 269.2 %collective-permute-start.1 = (f32[4,1,256]{2,1,0:T(1,128)S(1)}, f32[4,1,256]{2,1,0:T(1,128)S(1)}, u32[]{:S(2)}, u32[]{:S(2)}) collective-permute-start(f32[4,1,256]{2,1,0:T(1,128)S(1)} %get-tuple-element.300), channel_id=1, source_target_pairs={{0,1},{1,2},{2,3},{3,4},{4,5},{5,6},{6,7},{7,8},{8,9},{9,10},{10,1... | collective-permute-start | bytes 12296 | tf_op jit(solution)/shard_map/ppermute | solution.py:42
  2.0 268.6 %collective-permute-start = (f32[4,1,256]{2,1,0:T(1,128)S(1)}, f32[4,1,256]{2,1,0:T(1,128)S(1)}, u32[]{:S(2)}, u32[]{:S(2)}) collective-permute-start(f32[4,1,256]{2,1,0:T(1,128)S(1)} %get-tuple-element.299), channel_id=1, source_target_pairs={{1,0},{2,1},{3,2},{4,3},{5,4},{6,5},{7,6},{8,7},{9,8},{10,9},{11,1... | collective-permute-start | bytes 12296 | tf_op jit(solution)/shard_map/ppermute | solution.py:44
  61.0 170.1 %copy-start.1 = (f32[3,32,256]{2,1,0:T(8,128)S(1)}, f32[3,32,256]{2,1,0:T(8,128)}, u32[]{:S(2)}) copy-start(f32[3,32,256]{2,1,0:T(8,128)} %param.14) | copy-start | bytes 294916
  71.6 159.8 %copy-start.6 = (f32[32,256]{1,0:T(8,128)S(1)}, f32[32,256]{1,0:T(8,128)}, u32[]{:S(2)}) copy-start(f32[32,256]{1,0:T(8,128)} %param.15) | copy-start | bytes 98308
  71.6 159.9 %copy-start.2 = (f32[3,8192]{1,0:T(4,128)S(1)}, f32[3,8192]{1,0:T(4,128)}, u32[]{:S(2)}) copy-start(f32[3,8192]{1,0:T(4,128)} %param.19) | copy-start | bytes 294916
  80.0 190.6 %copy-start.5 = (f32[32,256]{1,0:T(8,128)S(1)}, f32[32,256]{1,0:T(8,128)}, u32[]{:S(2)}) copy-start(f32[32,256]{1,0:T(8,128)} %param.16) | copy-start | bytes 98308
  157.8 172.5 %all-to-all-start = ((s32[1,8,4,384]{3,2,0,1:T(4,128)}), s32[1,8,4,384]{3,2,0,1:T(4,128)S(1)}, u32[]{:S(2)}, u32[]{:S(2)}) async-start(s32[1,8,4,384]{3,2,0,1:T(4,128)} %reshape.154), calls=%async_computation | async-start | bytes 98304 | tf_op jit(solution)/shard_map/all_to_all | solution.py:144
  270.9 4.0 collective-permute-start.2
  273.6 6.6 %collective-permute-start.3 = (f32[3,1,256]{2,1,0:T(1,128)S(1)}, f32[3,1,256]{2,1,0:T(1,128)S(1)}, u32[]{:S(2)}, u32[]{:S(2)}) collective-permute-start(f32[3,1,256]{2,1,0:T(1,128)S(1)} %get-tuple-element.330), channel_id=1, source_target_pairs={{0,1},{1,2},{2,3},{3,4},{4,5},{5,6},{6,7},{7,8},{8,9},{9,10},{10,1... | collective-permute-start | bytes 9224 | tf_op jit(solution)/shard_map/ppermute | solution.py:42
  316.6 17.7 %collective-permute-start.4 = (f32[27,1,4,384]{3,2,0,1:T(4,128)}, f32[27,1,4,384]{3,2,0,1:T(4,128)}, u32[]{:S(2)}, u32[]{:S(2)}) collective-permute-start(f32[27,1,4,384]{3,2,0,1:T(4,128)} %bitcast.183), channel_id=1, source_target_pairs={{0,4},{4,0},{8,12},{12,8},{16,20},{20,16},{24,28},{28,24},{1,5},{5... | collective-permute-start | bytes 497672 | tf_op jit(solution)/shard_map/ppermute | solution.py:30
  319.3 16.0 %collective-permute-start.5 = (f32[27,1,4,384]{3,2,0,1:T(4,128)}, f32[27,1,4,384]{3,2,0,1:T(4,128)}, u32[]{:S(2)}, u32[]{:S(2)}) collective-permute-start(f32[27,1,4,384]{3,2,0,1:T(4,128)} %bitcast.61), channel_id=1, source_target_pairs={{0,8},{4,12},{8,0},{12,4},{16,24},{20,28},{24,16},{28,20},{1,9},{5... | collective-permute-start | bytes 497672 | tf_op jit(solution)/shard_map/ppermute | solution.py:30
  321.4 20.2 %collective-permute-start.6 = (f32[27,1,4,384]{3,2,0,1:T(4,128)}, f32[27,1,4,384]{3,2,0,1:T(4,128)}, u32[]{:S(2)}, u32[]{:S(2)}) collective-permute-start(f32[27,1,4,384]{3,2,0,1:T(4,128)} %bitcast.63), channel_id=1, source_target_pairs={{0,12},{4,8},{8,4},{12,0},{16,28},{20,24},{24,20},{28,16},{1,13},{... | collective-permute-start | bytes 497672 | tf_op jit(solution)/shard_map/ppermute | solution.py:30
  325.8 16.7 %collective-permute-start.7 = (f32[27,1,4,384]{3,2,0,1:T(4,128)}, f32[27,1,4,384]{3,2,0,1:T(4,128)}, u32[]{:S(2)}, u32[]{:S(2)}) collective-permute-start(f32[27,1,4,384]{3,2,0,1:T(4,128)} %bitcast.65), channel_id=1, source_target_pairs={{0,16},{4,20},{8,24},{12,28},{16,0},{20,4},{24,8},{28,12},{1,17},{... | collective-permute-start | bytes 497672 | tf_op jit(solution)/shard_map/ppermute | solution.py:30
  326.7 7.6 %copy-start.3 = (f32[8,27,1,4,384]{4,3,1,0,2:T(4,128)S(1)}, f32[8,27,1,4,384]{4,3,1,0,2:T(4,128)}, u32[]{:S(2)}) copy-start(f32[8,27,1,4,384]{4,3,1,0,2:T(4,128)} %bitcast_dynamic-update-slice_fusion.8) | copy-start | bytes 3981316
  326.7 16.8 %collective-permute-start.8 = (f32[27,1,4,384]{3,2,0,1:T(4,128)}, f32[27,1,4,384]{3,2,0,1:T(4,128)S(1)}, u32[]{:S(2)}, u32[]{:S(2)}) collective-permute-start(f32[27,1,4,384]{3,2,0,1:T(4,128)} %bitcast.67), channel_id=1, source_target_pairs={{0,20},{4,16},{8,28},{12,24},{16,4},{20,0},{24,12},{28,8},{1,21},{... | collective-permute-start | bytes 497672 | tf_op jit(solution)/shard_map/ppermute | solution.py:30
  330.9 19.7 %all-to-all-start.1 = ((s32[1,8,4,384]{3,1,0,2:T(8,128)}), s32[1,8,4,384]{3,1,0,2:T(8,128)S(1)}, u32[]{:S(2)}, u32[]{:S(2)}) async-start(s32[1,8,4,384]{3,1,0,2:T(8,128)} %copy.160), calls=%async_computation.1 | async-start | bytes 98304 | tf_op jit(solution)/shard_map/all_to_all | solution.py:143
  334.2 9.3 %collective-permute-start.9 = (f32[27,1,4,384]{3,2,0,1:T(4,128)}, f32[27,1,4,384]{3,2,0,1:T(4,128)S(1)}, u32[]{:S(2)}, u32[]{:S(2)}) collective-permute-start(f32[27,1,4,384]{3,2,0,1:T(4,128)} %bitcast.182), channel_id=1, source_target_pairs={{0,24},{4,28},{8,16},{12,20},{16,8},{20,12},{24,0},{28,4},{1,25},{... | collective-permute-start | bytes 497672 | tf_op jit(solution)/shard_map/ppermute | solution.py:30
  335.3 12.7 %collective-permute-start.10 = (f32[27,1,4,384]{3,2,0,1:T(4,128)S(1)}, f32[27,1,4,384]{3,2,0,1:T(4,128)S(1)}, u32[]{:S(2)}, u32[]{:S(2)}) collective-permute-start(f32[27,1,4,384]{3,2,0,1:T(4,128)S(1)} %bitcast.181), channel_id=1, source_target_pairs={{0,28},{4,24},{8,20},{12,16},{16,12},{20,8},{24,4},{28,0},{1,29},{... | collective-permute-start | bytes 497672 | tf_op jit(solution)/shard_map/ppermute | solution.py:30
  350.6 4.4 copy-start.4
  350.6 21.9 %all-to-all-start.2 = ((f32[27,8,4,384]{3,1,0,2:T(8,128)}), f32[27,8,4,384]{3,1,0,2:T(8,128)}, u32[]{:S(2)}, u32[]{:S(2)}) async-start(f32[27,8,4,384]{3,1,0,2:T(8,128)} %copy.171), calls=%async_computation.2 | async-start | bytes 2654208 | tf_op jit(solution)/shard_map/all_to_all | solution.py:134
  376.3 3.0 copy-start.7
  445.0 15.6 %all-to-all-start.3 = ((f32[3,8,4,384]{3,2,0,1:T(4,128)}), f32[3,8,4,384]{3,2,0,1:T(4,128)S(1)}, u32[]{:S(2)}, u32[]{:S(2)}) async-start(f32[3,8,4,384]{3,2,0,1:T(4,128)} %copy.176), calls=%async_computation.3 | async-start | bytes 294912 | tf_op jit(solution)/shard_map/all_to_all | solution.py:177
  461.3 90.2 %all-to-all-start.4 = ((f32[3,8,4,384]{3,1,0,2:T(8,128)}), f32[3,8,4,384]{3,1,0,2:T(8,128)S(1)}, u32[]{:S(2)}, u32[]{:S(2)}) async-start(f32[3,8,4,384]{3,1,0,2:T(8,128)} %copy.177), calls=%async_computation.4 | async-start | bytes 294912 | tf_op jit(solution)/shard_map/all_to_all | solution.py:176
